TPU v7x, 32 devices: a whole 2x2x4 slice. The times are simulated.
32 devices in a mesh: dp: 8 (over z, y), tr: 2 (over core), tc: 2 (over x).
Axes of the slice: x: 2, y: 2, z: 4, core: 2. Of those that a mesh axis runs over, the one named last changes fastest.
Arguments:
- activations: bfloat16 [4096, 4096], P('dp', ('tr', 'tc')), may hold values from -16.8 to 16.8, as said below
- gradients: bfloat16 [4096, 7168], P('dp', ('tr', 'tc')), may hold values from -16.8 to 16.8, as said below
- old_inputs: float32 [4096, 4096], P(('dp', 'tr', 'tc')), may hold values from -3 to 3
- old_gradients: float32 [7168, 7168], P(('dp', 'tr', 'tc')), may hold values from -3 to 3
Outputs:
- input_factor: float32 [4096, 4096], P(('dp', 'tr', 'tc'))
- grad_factor: float32 [7168, 7168], P(('dp', 'tr', 'tc'))
Inputs may be any that keep to these rules, and one draw needn't show every extreme that they name: `activations`: real-valued samples. `gradients`: real-valued samples.
All inputs are finite; a program needn't handle non-finite values.
Results may differ from a plain program's by a relative error of at most 0.0045.
Values may be sent and summed in bfloat16 or wider, within the bound.
A program may use at most 192 MiB of HBM per device.

v0:
```python
import functools

import jax
import jax.numpy as jnp
from jax import lax
from jax.experimental import pallas as pl
from jax.experimental.pallas import tpu as pltpu
from jax.sharding import Mesh, PartitionSpec as P

GROUP = (2, 2, 2)
REPLICA = ("q", "zh", "zl", "y")
AXES = REPLICA + ("tr", "tc")
F32, BF16 = jnp.float32, jnp.bfloat16
LANES, STEP = 128, 256
CHUNKS = (4, 2)


def split_mesh(mesh):
    size = mesh.shape["dp"] // 8
    rest = tuple(mesh.shape[name] for name in mesh.axis_names[1:])
    return Mesh(mesh.devices.reshape((size,) + GROUP + rest), AXES)


class Place:
    def __init__(self):
        for name in AXES:
            setattr(self, name, lax.axis_index(name))
        self.replica = self.zh * 4 + self.zl * 2 + self.y
        self.partner = self.zh * 4 + (1 - self.zl) * 2 + self.y

    def flip(self, *names):
        return {name: 1 - getattr(self, name) for name in names}


class Factor:
    def __init__(self, at, chunks, groups, samples, out, refs):
        self.at, self.chunks, self.groups = at, chunks, groups
        self.samples, self.out = samples, out
        (self.wide, self.left, self.left_in, self.pair, self.side, self.pair_in, self.side_in,
         self.total, self.local_sem, self.send_sem, self.recv_sem) = refs
        self.tokens, self.width = samples.shape
        self.rows = self.side.shape[0]
        self.half = 2 * self.width
        self.used, self.sent = {}, []

    def sem(self, *key):
        return self.used.setdefault(key, len(self.used))

    def spot(self, t, y, c, k):
        size = self.tokens // self.chunks
        row = pl.multiple_of((2 * t + y) * self.tokens + k * size, size)
        return self.wide.at[pl.ds(row, size), pl.ds(pl.multiple_of(c * self.width, LANES), self.width)]

    def own(self, k):
        size = self.tokens // self.chunks
        return self.samples.at[pl.ds(k * size, size)]

    def copy(self, key, source, target, device, recv=None):
        at = self.sem(*key)
        copy = pltpu.make_async_remote_copy(
            src_ref=source,
            dst_ref=target,
            send_sem=self.send_sem.at[at],
            recv_sem=self.recv_sem.at[at if recv is None else recv],
            device_id=device,
            device_id_type=pl.DeviceIdType.MESH,
        )
        return copy

    def start(self, *args):
        copy = self.copy(*args)
        copy.start()
        self.sent.append(copy)
        return copy

    def far(self, k):
        self.start(("far", k), self.own(k), self.spot(1, self.at.y, self.at.tc, k), self.at.flip("zh"))

    def far_wait(self, k):
        here = self.spot(1, self.at.y, self.at.tc, k)
        self.copy(("far", k), here, here, self.at.flip("zh")).wait_recv()

    def direct(self, t, k):
        here = self.spot(t, self.at.y, self.at.tc, k)
        source = here if t else self.own(k)
        for name in ("tc", "y"):
            self.start((name, t, k), source, here, self.at.flip(name))

    def direct_wait(self, t, k, name):
        y = self.at.y if name == "tc" else 1 - self.at.y
        c = 1 - self.at.tc if name == "tc" else self.at.tc
        here = self.spot(t, y, c, k)
        self.copy((name, t, k), here, here, self.at.flip(name)).wait_recv()
        return here

    def relay(self, t, k):
        first, then = (("tc", "y"), ("y", "tc"))[k % 2]
        here = self.direct_wait(t, k, first)
        self.start(("relay", t, k), here, here, self.at.flip(then))

    def rest_wait(self, t, k):
        self.direct_wait(t, k, ("y", "tc")[k % 2])
        here = self.spot(t, 1 - self.at.y, 1 - self.at.tc, k)
        self.copy(("relay", t, k), here, here, self.at.flip("y")).wait_recv()

    def local(self):
        y, c = self.at.y, self.at.tc
        row = pl.multiple_of(y * self.tokens, self.tokens)
        target = self.wide.at[
            pl.ds(row, self.tokens), pl.ds(pl.multiple_of(c * self.width, LANES), self.width)
        ]
        return pltpu.make_async_copy(self.samples, target, self.local_sem.at[0])

    def pick_left(self, groups_rows):
        at, rows = self.at, self.rows
        each = groups_rows
        span = 4 * each
        window = span if span % LANES == 0 else -(-span // LANES) * LANES + LANES
        features = lax.broadcasted_iota(jnp.int32, (rows, window), 1)
        line = lax.broadcasted_iota(jnp.int32, (rows, window), 0)
        for s, replica in ((0, at.replica), (1, at.partner)):
            picks, starts = [], []
            for group in range(self.groups):
                offset = (group * 8 + replica) * span - at.tr * self.half
                start = jnp.clip(offset // LANES * LANES, 0, self.half - window)
                starts.append(pl.multiple_of(start, LANES))
                for core in range(2):
                    wanted = offset + (core * 2 + at.tc) * each - group * each - start
                    hit = features == line + wanted
                    if self.groups > 1:
                        hit &= (line >= group * each) & (line < (group + 1) * each)
                    picks.append(jnp.where(hit, 1.0, 0.0).astype(BF16))

            for core in range(2):
                def block(b, carry, s=s, core=core, picks=picks, starts=starts):
                    tokens = pl.ds(pl.multiple_of(b * self.tokens, self.tokens), self.tokens)
                    total = jnp.zeros((rows, self.tokens), F32)
                    for group in range(self.groups):
                        total += lax.dot_general(
                            picks[2 * group + core],
                            self.wide[tokens, pl.ds(starts[group], window)],
                            (((1,), (1,)), ((), ())),
                            preferred_element_type=F32,
                        )
                    self.left[s, core * rows:(core + 1) * rows, tokens] = total.astype(BF16)
                    return carry

                lax.fori_loop(0, 4, block, 0)

    def make_left(self, groups_rows):
        other = self.at.flip("tr")
        if self.groups == 1:
            mine = self.at.tr == self.at.zh
            copy = self.copy(("left",), self.left, self.left, other)

            @pl.when(mine)
            def _():
                self.pick_left(groups_rows)
                copy.start()

            @pl.when(jnp.logical_not(mine))
            def _():
                copy.wait_recv()

            self.left_copy = (mine, copy)
        else:
            self.pick_left(groups_rows)
            copy = self.copy(("left",), self.left, self.left_in, other)
            copy.start()
            copy.wait()
            self.left[...] = self.left[...] + self.left_in[...]
            self.left_copy = None

    def products(self, scale):
        at, rows, width = self.at, self.rows, self.width
        for part in range(2):
            def pair(i, carry, part=part):
                columns = pl.ds(pl.multiple_of(part * width + i * STEP, STEP), STEP)
                product = jnp.dot(self.left[1], self.wide[:, columns], preferred_element_type=F32)
                self.pair[:, columns] = (product * scale).astype(BF16)
                return carry

            lax.fori_loop(0, width // STEP, pair, 0)
            columns = pl.ds(part * width, width)
            for core in range(2):
                device = dict(at.flip("zl"), tr=core)
                self.start(
                    ("pair", part, core),
                    self.pair.at[pl.ds(core * rows, rows), columns],
                    self.pair_in.at[at.tr, :, columns],
                    device,
                    self.pair_slot(part, at.tr),
                )
        mine = pl.ds(pl.multiple_of(at.tr * rows, 16), rows)
        others = pl.ds(pl.multiple_of((1 - at.tr) * rows, 16), rows)

        def side(i, carry):
            columns = pl.ds(pl.multiple_of(i * STEP, STEP), STEP)
            product = jnp.dot(self.left[0, others, :], self.wide[:, columns], preferred_element_type=F32)
            self.side[:, columns] = (product * scale).astype(BF16)
            return carry

        lax.fori_loop(0, self.half // STEP, side, 0)
        self.start(("side",), self.side, self.side_in, at.flip("tr"))

        def own(i, carry):
            columns = pl.ds(pl.multiple_of(i * STEP, STEP), STEP)
            product = jnp.dot(self.left[0, mine, :], self.wide[:, columns], preferred_element_type=F32)
            place = pl.ds(pl.multiple_of(at.tr * self.half + i * STEP, STEP), STEP)
            self.total[:, place] = product * scale
            return carry

        lax.fori_loop(0, self.half // STEP, own, 0)

    def pair_slot(self, part, core):
        return self.sem("pair", part, 0) + core

    def finish(self):
        at = self.at
        self.copy(("side",), self.side, self.side_in, at.flip("tr")).wait_recv()

        def side(i, carry):
            columns = pl.ds(pl.multiple_of(i * STEP, STEP), STEP)
            place = pl.ds(pl.multiple_of((1 - at.tr) * self.half + i * STEP, STEP), STEP)
            self.total[:, place] = self.side_in[:, columns].astype(F32)
            return carry

        lax.fori_loop(0, self.half // STEP, side, 0)
        outs = []
        for part in range(2):
            for core in range(2):
                here = self.pair_in.at[core, :, pl.ds(part * self.width, self.width)]
                self.copy(("pair", part, core), here, here, dict(at.flip("zl"))).wait_recv()

                def add(i, carry, part=part, core=core):
                    columns = pl.ds(pl.multiple_of(part * self.width + i * STEP, STEP), STEP)
                    place = pl.ds(pl.multiple_of(core * self.half + part * self.width + i * STEP, STEP), STEP)
                    self.total[:, place] += self.pair_in[core, :, columns].astype(F32)
                    return carry

                lax.fori_loop(0, self.width // STEP, add, 0)
                place = pl.ds(core * self.half + part * self.width, self.width)
                copy = pltpu.make_async_copy(
                    self.total.at[:, place], self.out.at[:, place], self.local_sem.at[1 + 2 * part + core]
                )
                copy.start()
                outs.append(copy)
        return outs

    def drain(self):
        for copy in self.sent:
            copy.wait_send()
        if self.left_copy is not None:
            mine, copy = self.left_copy

            @pl.when(mine)
            def _():
                copy.wait_send()


def kernel(groups, each, scale, grads, acts, out_g, out_a, *scratch):
    at = Place()
    barrier = pltpu.get_barrier_semaphore()
    peers = [at.flip(name) for name in ("tc", "y", "zh", "tr")]
    peers += [dict(at.flip("zl"), tr=core) for core in range(2)]
    for peer in peers:
        pl.semaphore_signal(barrier, inc=1, device_id=peer, device_id_type=pl.DeviceIdType.MESH)
    pl.semaphore_wait(barrier, len(peers))

    count = len(scratch) // 2
    g = Factor(at, CHUNKS[0], groups, grads, out_g, scratch[:count])
    a = Factor(at, CHUNKS[1], groups, acts, out_a, scratch[count:])

    for factor in (g, a):
        for k in range(factor.chunks):
            factor.far(k)
    for k in range(g.chunks):
        g.direct(0, k)
    locals_ = [factor.local() for factor in (g, a)]
    for copy in locals_:
        copy.start()

    half = g.chunks // 2
    for k in range(half):
        g.relay(0, k)
    g.far_wait(0)
    g.direct(1, 0)
    for k in range(half, g.chunks):
        g.relay(0, k)
    for k in range(1, g.chunks):
        g.far_wait(k)
        g.direct(1, k)
        if k >= 2:
            g.relay(1, k - 2)
    for k in range(g.chunks - 2, g.chunks):
        g.relay(1, k)
    for k in range(a.chunks):
        a.direct(0, k)
    for copy in locals_:
        copy.wait()
    for t in range(2):
        for k in range(g.chunks):
            g.rest_wait(t, k)
    g.make_left(each[0])
    g.products(scale)
    for k in range(a.chunks):
        a.far_wait(k)
        a.direct(1, k)
    for t in range(2):
        for k in range(a.chunks):
            a.relay(t, k)
    for t in range(2):
        for k in range(a.chunks):
            a.rest_wait(t, k)
    a.make_left(each[1])
    a.products(scale)
    outs = g.finish() + a.finish()
    for factor in (g, a):
        factor.drain()
    for copy in outs:
        copy.wait()


def scratch_of(samples, rows, groups, chunks):
    tokens, width = samples.shape
    half = 2 * width
    left = pltpu.VMEM((2, 2 * rows, 4 * tokens), BF16)
    copies = 7 * chunks + 6
    return [
        pltpu.VMEM((4 * tokens, half), BF16),
        left,
        left if groups > 1 else pltpu.VMEM((16, LANES), BF16),
        pltpu.VMEM((2 * rows, half), BF16),
        pltpu.VMEM((rows, half), BF16),
        pltpu.VMEM((2, rows, half), BF16),
        pltpu.VMEM((rows, half), BF16),
        pltpu.VMEM((rows, 2 * half), F32),
        pltpu.SemaphoreType.DMA((5,)),
        pltpu.SemaphoreType.DMA((copies,)),
        pltpu.SemaphoreType.DMA((copies,)),
    ]


def body(activations, gradients, old_inputs, old_gradients):
    groups = lax.axis_size("q")
    tokens = activations.shape[0] * lax.axis_size(REPLICA)
    samples, olds = (gradients, activations), (old_gradients, old_inputs)
    each = tuple(old.shape[0] for old in olds)
    scratch = []
    for block, rows, chunks in zip(samples, each, CHUNKS):
        scratch += scratch_of(block, groups * rows, groups, chunks)
    new = pl.pallas_call(
        functools.partial(kernel, groups, each, 1.0 / tokens),
        out_shape=tuple(
            jax.ShapeDtypeStruct((groups * old.shape[0], old.shape[1]), F32) for old in olds
        ),
        in_specs=[pl.BlockSpec(memory_space=pltpu.HBM)] * 2,
        out_specs=(pl.BlockSpec(memory_space=pltpu.HBM),) * 2,
        scratch_shapes=scratch,
        compiler_params=pltpu.CompilerParams(
            collective_id=0, has_side_effects=True, vmem_limit_bytes=60 * 2**20
        ),
        name="gram",
    )(*samples)
    outs = []
    for total, old in zip(new, olds):
        if groups > 1:
            total = lax.psum_scatter(total, "q", scatter_dimension=0, tiled=True)
        outs.append(0.5 * old + 0.5 * total)
    return outs[1], outs[0]


def solution(mesh):
    rows = REPLICA + ("tr", "tc")
    return jax.shard_map(
        body,
        mesh=split_mesh(mesh),
        in_specs=(
            P(REPLICA, ("tr", "tc")),
            P(REPLICA, ("tr", "tc")),
            P(rows, None),
            P(rows, None),
        ),
        out_specs=(P(rows, None), P(rows, None)),
        check_vma=False,
    )
```

profile of v0, /device:TPU:17, one launch (start us, length us, event | category | flops | bytes accessed | tf_op | source)
XLA Modules:
  0.0 266.8 jit_solution(5351986418311150596)
XLA Ops:
  0.6 0.0 copy-start
  0.6 254.4 %gram.1 = (f32[224,7168]{1,0:T(8,128)}, f32[128,4096]{1,0:T(8,128)}) custom-call(bf16[512,1792]{1,0:T(8,128)(2,1)} %grads.1, bf16[512,1024]{1,0:T(8,128)(2,1)} %acts.1), custom_call_target="tpu_custom_call" | custom-call | tf_op jit(solution)/shard_map/gram/pallas_call | solution.py:352
  255.1 0.0 copy-done
  255.1 3.2 %add_multiply_fusion.1 = f32[128,4096]{1,0:T(8,128)} fusion(f32[128,4096]{1,0:T(8,128)S(1)} %copy-done, f32[128,4096]{1,0:T(8,128)} %get-tuple-element.4), kind=kLoop, calls=%fused_computation.1 | loop fusion | flops 1048576 | bytes 6291456 | tf_op jit(solution)/shard_map/add | solution.py:369
  258.2 8.5 %add_multiply_fusion = f32[224,7168]{1,0:T(8,128)} fusion(f32[224,7168]{1,0:T(8,128)} %param.7, f32[224,7168]{1,0:T(8,128)} %get-tuple-element.5), kind=kLoop, calls=%fused_computation | loop fusion | flops 3211264 | bytes 19267584 | tf_op jit(solution)/shard_map/add | solution.py:369
Async XLA Ops:
  0.6 254.4 %copy-start = (f32[128,4096]{1,0:T(8,128)S(1)}, f32[128,4096]{1,0:T(8,128)}, u32[]{:S(2)}) copy-start(f32[128,4096]{1,0:T(8,128)} %param.6) | copy-start | bytes 6291460
where the time goes:
time: 272 us; the launch traced here: 267 us
  Pallas kernels  254 us (93%)
  other arithmetic  11.7 us (4%)
    pallas_call x1, Pallas kernels, body(): pl.pallas_call(functools.partial(kernel, groups, each, 1.0 / tokens), out...  254 us
    add x2, other arithmetic, body(): outs.append(0.5 * old + 0.5 * total)  11.7 us

commit v1 on v0

v1 whole, which is shorter than its diff:
```python
import functools

import jax
import jax.numpy as jnp
from jax import lax
from jax.experimental import pallas as pl
from jax.experimental.pallas import tpu as pltpu
from jax.sharding import Mesh, PartitionSpec as P

GROUP = (2, 2, 2)
REPLICA = ("q", "zh", "zl", "y")
AXES = REPLICA + ("tr", "tc")
F32, BF16 = jnp.float32, jnp.bfloat16
LANES, STEP, VMEM = 128, 256, 60 * 2**20
CHUNKS = (4, 2)


def split_mesh(mesh):
    size = mesh.shape["dp"] // 8
    rest = tuple(mesh.shape[name] for name in mesh.axis_names[1:])
    return Mesh(mesh.devices.reshape((size,) + GROUP + rest), AXES)


class Place:
    def __init__(self):
        for name in AXES:
            setattr(self, name, lax.axis_index(name))
        self.replica = self.zh * 4 + self.zl * 2 + self.y
        self.partner = self.zh * 4 + (1 - self.zl) * 2 + self.y

    def flip(self, *names):
        return {name: 1 - getattr(self, name) for name in names}


class Factor:
    def __init__(self, at, chunks, groups, each, samples, old, total, refs):
        self.at, self.chunks, self.groups, self.each = at, chunks, groups, each
        self.samples, self.old, self.total = samples, old, total
        (self.wide, self.left, self.left_in, self.pair, self.side, self.pair_in, self.side_in,
         self.block, self.local_sem, self.send_sem, self.recv_sem) = refs
        self.tokens, self.width = samples.shape
        self.rows = self.side.shape[0]
        self.half = 2 * self.width
        self.fold = groups == 1
        keys = [("far", k) for k in range(chunks)]
        keys += [(n, t, k) for n in ("tc", "y", "relay") for t in range(2) for k in range(chunks)]
        keys += [("left", t) for t in range(2)] + [("side",)]
        keys += [("pair", part, core) for part in range(2) for core in range(2)]
        self.keys = {key: i for i, key in enumerate(keys)}
        self.sent, self.far_sent, self.left_sent = [], [], []

    def sem(self, *key):
        return self.keys[key]

    def spot(self, t, y, c, k):
        size = self.tokens // self.chunks
        row = pl.multiple_of((2 * t + y) * self.tokens + k * size, size)
        return self.wide.at[pl.ds(row, size), pl.ds(pl.multiple_of(c * self.width, LANES), self.width)]

    def own(self, k):
        size = self.tokens // self.chunks
        return self.samples.at[pl.ds(k * size, size)]

    def copy(self, key, source, target, device, recv=None):
        at = self.sem(*key)
        copy = pltpu.make_async_remote_copy(
            src_ref=source,
            dst_ref=target,
            send_sem=self.send_sem.at[at],
            recv_sem=self.recv_sem.at[at if recv is None else recv],
            device_id=device,
            device_id_type=pl.DeviceIdType.MESH,
        )
        return copy

    def start(self, *args):
        copy = self.copy(*args)
        copy.start()
        self.sent.append(copy)
        return copy

    def far(self, k):
        here = self.spot(1, self.at.y, self.at.tc, k)
        self.far_sent.append(self.start(("far", k), self.own(k), here, self.at.flip("zh")))

    def far_left(self):
        for copy in self.far_sent:
            copy.wait_send()
        self.sent = [copy for copy in self.sent if not any(copy is one for one in self.far_sent)]

    def far_wait(self, k):
        here = self.spot(1, self.at.y, self.at.tc, k)
        self.copy(("far", k), here, here, self.at.flip("zh")).wait_recv()

    def direct(self, t, k):
        here = self.spot(t, self.at.y, self.at.tc, k)
        source = here if t else self.own(k)
        for name in ("tc", "y"):
            self.start((name, t, k), source, here, self.at.flip(name))

    def direct_wait(self, t, k, name):
        y = self.at.y if name == "tc" else 1 - self.at.y
        c = 1 - self.at.tc if name == "tc" else self.at.tc
        here = self.spot(t, y, c, k)
        self.copy((name, t, k), here, here, self.at.flip(name)).wait_recv()
        return here

    def relay(self, t, k):
        first, then = (("tc", "y"), ("y", "tc"))[k % 2]
        here = self.direct_wait(t, k, first)
        self.start(("relay", t, k), here, here, self.at.flip(then))

    def rest_wait(self, t, k):
        self.direct_wait(t, k, ("y", "tc")[k % 2])
        here = self.spot(t, 1 - self.at.y, 1 - self.at.tc, k)
        self.copy(("relay", t, k), here, here, self.at.flip("y")).wait_recv()

    def local(self):
        y, c = self.at.y, self.at.tc
        row = pl.multiple_of(y * self.tokens, self.tokens)
        target = self.wide.at[
            pl.ds(row, self.tokens), pl.ds(pl.multiple_of(c * self.width, LANES), self.width)
        ]
        copies = [pltpu.make_async_copy(self.samples, target, self.local_sem.at[0])]
        if self.fold:
            copies.append(pltpu.make_async_copy(self.old, self.total, self.local_sem.at[1]))
        return copies

    def pick_left(self, t):
        at, rows, each = self.at, self.rows, self.each
        span = 4 * each
        window = span if span % LANES == 0 else -(-span // LANES) * LANES + LANES
        features = lax.broadcasted_iota(jnp.int32, (rows, window), 1)
        line = lax.broadcasted_iota(jnp.int32, (rows, window), 0)
        for s, replica in ((0, at.replica), (1, at.partner)):
            picks, starts = [], []
            for group in range(self.groups):
                offset = (group * 8 + replica) * span - at.tr * self.half
                start = jnp.clip(offset // LANES * LANES, 0, self.half - window)
                starts.append(pl.multiple_of(start, LANES))
                both = []
                for core in range(2):
                    wanted = offset + (core * 2 + at.tc) * each - group * each - start
                    hit = features == line + wanted
                    if self.groups > 1:
                        hit &= (line >= group * each) & (line < (group + 1) * each)
                    both.append(jnp.where(hit, 1.0, 0.0).astype(BF16))
                picks.append(jnp.concatenate(both, axis=0))

            def block(b, carry, s=s, picks=picks, starts=starts):
                tokens = pl.ds(pl.multiple_of((2 * t + b) * self.tokens, self.tokens), self.tokens)
                total = 0.0
                for pick, start in zip(picks, starts):
                    total += lax.dot_general(
                        pick,
                        self.wide[tokens, pl.ds(start, window)],
                        (((1,), (1,)), ((), ())),
                        preferred_element_type=F32,
                    )
                self.left[s, :, tokens] = total.astype(BF16)
                return carry

            lax.fori_loop(0, 2, block, 0)

    def left_copy(self, t):
        tokens = pl.ds(2 * t * self.tokens, 2 * self.tokens)
        target = self.left if self.groups == 1 else self.left_in
        return ("left", t), self.left.at[:, :, tokens], target.at[:, :, tokens], self.at.flip("tr")

    def make_left(self, t, mine):
        if mine or self.groups > 1:
            self.pick_left(t)
            self.left_sent.append(self.start(*self.left_copy(t)))

    def get_left(self, mine):
        if not mine or self.groups > 1:
            for t in range(2):
                self.copy(*self.left_copy(t)).wait_recv()
        if self.groups > 1:
            for copy in self.left_sent:
                copy.wait_send()
            self.sent = [copy for copy in self.sent if not any(copy is one for one in self.left_sent)]
            self.left[...] = self.left[...] + self.left_in[...]

    def product(self, s, columns):
        return jnp.dot(self.left[s], self.wide[:, columns], preferred_element_type=F32)

    def pair_products(self, scale):
        at, rows, width = self.at, self.rows, self.width
        for part in range(2):
            def pair(i, carry, part=part):
                columns = pl.ds(pl.multiple_of(part * width + i * STEP, STEP), STEP)
                self.pair[:, columns] = (self.product(1, columns) * scale).astype(BF16)
                return carry

            lax.fori_loop(0, width // STEP, pair, 0)
            columns = pl.ds(part * width, width)
            for core in range(2):
                self.start(
                    ("pair", part, core),
                    self.pair.at[pl.ds(core * rows, rows), columns],
                    self.pair_in.at[at.tr, :, columns],
                    dict(at.flip("zl"), tr=core),
                    self.sem("pair", part, 0) + at.tr,
                )

    def add(self, place, value, first):
        if self.fold:
            base = 0.5 * self.total[:, place] if first else self.total[:, place]
            self.total[:, place] = base + 0.5 * value
        elif first:
            self.total[:, place] = value
        else:
            self.total[:, place] += value

    def own_products(self, scale):
        at, rows = self.at, self.rows
        mine = pl.ds(pl.multiple_of(at.tr * rows, 16), rows)
        others = pl.ds(pl.multiple_of((1 - at.tr) * rows, 16), rows)

        def own(i, carry):
            columns = pl.ds(pl.multiple_of(i * STEP, STEP), STEP)
            place = pl.ds(pl.multiple_of(at.tr * self.half + i * STEP, STEP), STEP)
            self.block[...] = self.product(0, columns) * scale
            self.side[:, columns] = self.block[others, :].astype(BF16)
            self.add(place, self.block[mine, :], True)
            return carry

        lax.fori_loop(0, self.half // STEP, own, 0)
        self.start(("side",), self.side, self.side_in, at.flip("tr"))

    def finish(self):
        at = self.at
        self.copy(("side",), self.side, self.side_in, at.flip("tr")).wait_recv()

        def side(i, carry):
            columns = pl.ds(pl.multiple_of(i * STEP, STEP), STEP)
            place = pl.ds(pl.multiple_of((1 - at.tr) * self.half + i * STEP, STEP), STEP)
            self.add(place, self.side_in[:, columns].astype(F32), True)
            return carry

        lax.fori_loop(0, self.half // STEP, side, 0)
        for core in range(2):
            for part in range(2):
                here = self.pair_in.at[core, :, pl.ds(part * self.width, self.width)]
                self.copy(("pair", part, core), here, here, at.flip("zl")).wait_recv()

                def add(i, carry, part=part, core=core):
                    columns = pl.ds(pl.multiple_of(part * self.width + i * STEP, STEP), STEP)
                    place = pl.ds(pl.multiple_of(core * self.half + part * self.width + i * STEP, STEP), STEP)
                    self.add(place, self.pair_in[core, :, columns].astype(F32), False)
                    return carry

                lax.fori_loop(0, self.width // STEP, add, 0)

    def drain(self):
        for copy in self.sent:
            copy.wait_send()


def program(lead, at, g, a, scale, flags):
    def tell(i):
        pl.semaphore_signal(flags.at[i], inc=1, device_id=at.flip("tr"), device_id_type=pl.DeviceIdType.MESH)

    def hear(i):
        pl.semaphore_wait(flags.at[i], 1)

    def each(factor, call, *args):
        for k in range(factor.chunks):
            call(*args, k)

    if not lead:
        each(g, g.far)
    each(g, g.direct, 0)
    local = [copy for factor in (g, a) for copy in factor.local()]
    for copy in local:
        copy.start()
    each(g, g.relay, 0)
    for copy in local:
        copy.wait()
    if lead:
        for k in range(g.chunks):
            g.far_wait(k)
            g.direct(1, k)
        hear(0)
        each(g, g.far)
        each(g, g.rest_wait, 0)
        g.make_left(0, lead)
        each(g, g.relay, 1)
        each(g, g.rest_wait, 1)
        tell(1)
        g.make_left(1, lead)
        g.get_left(lead)
        g.pair_products(scale)
        g.own_products(scale)
        each(a, a.direct, 0)
        hear(2)
        each(a, a.far)
        each(a, a.relay, 0)
        for k in range(a.chunks):
            a.far_wait(k)
            a.direct(1, k)
        each(a, a.rest_wait, 0)
        a.make_left(0, lead)
        each(a, a.relay, 1)
        each(a, a.rest_wait, 1)
        tell(3)
        a.make_left(1, lead)
        a.get_left(lead)
        a.pair_products(scale)
        a.own_products(scale)
    else:
        g.far_left()
        tell(0)
        each(g, g.rest_wait, 0)
        g.make_left(0, lead)
        each(g, g.far_wait)
        each(a, a.far)
        hear(1)
        each(g, g.direct, 1)
        each(g, g.relay, 1)
        each(a, a.direct, 0)
        a.far_left()
        tell(2)
        each(g, g.rest_wait, 1)
        g.make_left(1, lead)
        g.get_left(lead)
        g.pair_products(scale)
        each(a, a.relay, 0)
        g.own_products(scale)
        each(a, a.far_wait)
        each(a, a.rest_wait, 0)
        a.make_left(0, lead)
        hear(3)
        each(a, a.direct, 1)
        each(a, a.relay, 1)
        each(a, a.rest_wait, 1)
        a.make_left(1, lead)
        a.get_left(lead)
        a.pair_products(scale)
        a.own_products(scale)
    g.finish()
    a.finish()
    g.drain()
    a.drain()


def kernel(groups, each, scale, *refs):
    at = Place()
    barrier = pltpu.get_barrier_semaphore()
    peers = [at.flip(name) for name in ("tc", "y", "zh", "tr")]
    peers += [dict(at.flip("zl"), tr=core) for core in range(2)]
    for peer in peers:
        pl.semaphore_signal(barrier, inc=1, device_id=peer, device_id_type=pl.DeviceIdType.MESH)
    pl.semaphore_wait(barrier, len(peers))

    samples, refs = refs[:2], refs[2:]
    olds = (None, None)
    if groups == 1:
        olds, refs = refs[:2], refs[2:]
    totals, scratch, flags = refs[:2], refs[2:-1], refs[-1]
    count = len(scratch) // 2

    def run(lead):
        factors = [
            Factor(at, CHUNKS[i], groups, each[i], samples[i], olds[i], totals[i],
                   scratch[i * count:(i + 1) * count])
            for i in range(2)
        ]
        program(lead, at, *factors, scale, flags)

    lead = at.tr == at.zh
    pl.when(lead)(functools.partial(run, True))
    pl.when(jnp.logical_not(lead))(functools.partial(run, False))


def scratch_of(samples, rows, groups, chunks):
    tokens, width = samples.shape
    half = 2 * width
    left = pltpu.VMEM((2, 2 * rows, 4 * tokens), BF16)
    copies = 7 * chunks + 7
    return [
        pltpu.VMEM((4 * tokens, half), BF16),
        left,
        left if groups > 1 else pltpu.VMEM((16, LANES), BF16),
        pltpu.VMEM((2 * rows, half), BF16),
        pltpu.VMEM((rows, half), BF16),
        pltpu.VMEM((2, rows, half), BF16),
        pltpu.VMEM((rows, half), BF16),
        pltpu.VMEM((2 * rows, STEP), F32),
        pltpu.SemaphoreType.DMA((2,)),
        pltpu.SemaphoreType.DMA((copies,)),
        pltpu.SemaphoreType.DMA((copies,)),
    ]


def body(activations, gradients, old_inputs, old_gradients):
    groups = lax.axis_size("q")
    tokens = activations.shape[0] * lax.axis_size(REPLICA)
    samples, olds = (gradients, activations), (old_gradients, old_inputs)
    each = tuple(old.shape[0] for old in olds)
    scratch = []
    for block, rows, chunks in zip(samples, each, CHUNKS):
        scratch += scratch_of(block, groups * rows, groups, chunks)
    scratch.append(pltpu.SemaphoreType.REGULAR((4,)))
    operands = samples + olds if groups == 1 else samples
    new = pl.pallas_call(
        functools.partial(kernel, groups, each, 1.0 / tokens),
        out_shape=tuple(
            jax.ShapeDtypeStruct((groups * old.shape[0], old.shape[1]), F32) for old in olds
        ),
        in_specs=[pl.BlockSpec(memory_space=pltpu.HBM)] * len(operands),
        out_specs=(pl.BlockSpec(memory_space=pltpu.VMEM),) * 2,
        scratch_shapes=scratch,
        compiler_params=pltpu.CompilerParams(
            collective_id=0, has_side_effects=True, vmem_limit_bytes=VMEM
        ),
        name="gram",
    )(*operands)
    if groups > 1:
        new = [lax.psum_scatter(total, "q", scatter_dimension=0, tiled=True) for total in new]
        new = [0.5 * old + 0.5 * total for total, old in zip(new, olds)]
    return new[1], new[0]


def solution(mesh):
    rows = REPLICA + ("tr", "tc")
    return jax.shard_map(
        body,
        mesh=split_mesh(mesh),
        in_specs=(
            P(REPLICA, ("tr", "tc")),
            P(REPLICA, ("tr", "tc")),
            P(rows, None),
            P(rows, None),
        ),
        out_specs=(P(rows, None), P(rows, None)),
        check_vma=False,
    )
```

time: 272 us -> 234 us (0.86); the launches traced: 267 us -> 234 us
  Pallas kernels: 254 us -> 224 us
  other arithmetic: 11.7 us -> 0 us
  local copies, waits for them, and re-layouts: 0.01 us -> 9.39 us
    pallas_call x1, Pallas kernels: 254 us -> 224 us  [body(): pl.pallas_call(functools.partial(kernel, groups, each, 1.0 / tokens), out...]
    add x2 -> x0, other arithmetic: 11.7 us -> none  [body(): outs.append(0.5 * old + 0.5 * total)]
    unnamed x2, local copies, waits for them, and re-layouts: 0.01 us -> 9.39 us
where the time goes in v1:
time: 234 us
  Pallas kernels  224 us (96%)
  local copies, waits for them, and re-layouts  9.39 us (4%)
    pallas_call x1, Pallas kernels, body(): pl.pallas_call(functools.partial(kernel, groups, each, 1.0 / tokens), out...  224 us
    unnamed x2, local copies, waits for them, and re-layouts  9.39 us

profile of v1, /device:TPU:17, one launch (start us, length us, event | category | flops | bytes accessed | tf_op | source)
XLA Modules:
  0.0 233.6 jit_solution(5162089734957476456)
XLA Ops:
  0.6 223.6 %gram.1 = (f32[224,7168]{1,0:T(8,128)}, f32[128,4096]{1,0:T(8,128)}) custom-call(bf16[512,1792]{1,0:T(8,128)(2,1)} %refs_0_.1, bf16[512,1024]{1,0:T(8,128)(2,1)} %refs_1_.1, f32[224,7168]{1,0:T(8,128)} %refs_2_.1, f32[128,4096]{1,0:T(8,128)} %refs_3_.1), custom_call_target="tpu_custom_call" | custom-call | tf_op jit(solution)/shard_map/gram/pallas_call | solution.py:407
  224.3 3.1 %copy.8 = f32[128,4096]{1,0:T(8,128)} copy(f32[128,4096]{1,0:T(8,128)} %get-tuple-element.8) | data formatting | bytes 4194304
  227.4 6.3 %copy.9 = f32[224,7168]{1,0:T(8,128)} copy(f32[224,7168]{1,0:T(8,128)} %get-tuple-element.9) | data formatting | bytes 12845056
